TPU v7x, 512 devices: a whole 4x8x8 slice. The times are simulated.
512 devices in a mesh: slab: 64 (over z, x, core), tile: 8 (over y).
Axes of the slice: x: 4, y: 8, z: 8, core: 2. Of those that a mesh axis runs over, the one named last changes fastest.
Arguments:
- features: bfloat16 [64, 8, 512, 128], P('slab', 'tile'), may hold values from -24 to 24
- counts: int32 [64, 8], P('slab', 'tile'), may hold values from 128 to 512, as said below
- rulebook: int32 [64, 8, 27, 512], P('slab', 'tile'), may hold values from 0 to 800, as said below
- face_rows: int32 [64, 8, 4, 64], P('slab', 'tile'), may hold values from 0 to 511, as said below
- conv_one: bfloat16 [27, 128, 128], replicated, may hold values from -0.109375 to 0.109375
- gain_one: float32 [128], replicated, may hold values from 0.5 to 1.5
- shift_one: float32 [128], replicated, may hold values from -0.5 to 0.5
- conv_two: bfloat16 [27, 128, 128], replicated, may hold values from -0.109375 to 0.109375
- gain_two: float32 [128], replicated, may hold values from 0.5 to 1.5
- shift_two: float32 [128], replicated, may hold values from -0.5 to 0.5
Outputs:
- output: bfloat16 [64, 8, 512, 128], P('slab', 'tile')
Inputs may be any that keep to these rules, and one draw needn't show every extreme that they name: `counts`: each device's voxels fill its 8 x 8 grid columns with the same number each, between 2 and 8; some device of the highest slab index holds 512. `rulebook`: an entry names the extended-table row that holds the voxel's neighbour at offset k = 9 (dx + 1) + 3 (dy + 1) + (dz + 1) of the submanifold 3x3x3 stencil, or 800 where that cell is inactive or outside the grid; the voxel itself is at offset 13; rows at or past the device's count name 800 at every offset. `face_rows`: lists 0 to 3 hold the device's voxels on its lower and higher face along the first, then the lower and higher face along the second dimension; the j-th voxel of the i-th column along a face stands at position i * 8 + j; unused positions name row 0.
All inputs are finite; a program needn't handle non-finite values.
Results may differ from a plain program's by a relative error of at most 0.0033.
Values may be sent and summed in bfloat16 or wider, within the bound.
No kernel may reach another device: no remote copies, remote signals or barrier semaphores. Data moves between devices by JAX's collectives and lax.ppermute only.
A program may use at most 64 MiB of HBM per device.

v0:
```python
from functools import partial
import jax
import jax.numpy as jnp
from jax import lax
from jax.sharding import Mesh
from jax.sharding import PartitionSpec as P

SIDE = 8
SLAB = ("slab_0", "slab_1", "slab_2")
SLAB_TILE = ("slab_0", "slab_1", "slab_2", "tile")
EPSILON = 1e-05


def extended(block, sides, width):
    for axis, dim in sides:
        count = lax.axis_size(axis)
        forward = [(i, i + 1) for i in range(count - 1)]
        backward = [(target, source) for source, target in forward]
        low = lax.ppermute(
            lax.slice_in_dim(block, block.shape[dim] - width, None, axis=dim), axis, forward
        )
        high = lax.ppermute(lax.slice_in_dim(block, 0, width, axis=dim), axis, backward)
        block = jnp.concatenate([low, block, high], axis=dim)
    return block


def by_axis(shard, axes):
    for axis in axes:
        shard = lax.psum(shard, axis)
    return shard


def build_table(local_rows, face_lists):
    face_len = face_lists.shape[1]
    column = face_len // SIDE
    picked = local_rows[face_lists]
    tile_recv = extended(picked[2:4], (("tile", 0),), 1)
    core_low = tile_recv[0]
    core_high = tile_recv[3]
    slab_send = jnp.stack(
        [
            jnp.concatenate([picked[0], core_low[:column], core_high[:column]], axis=0),
            jnp.concatenate(
                [picked[1], core_low[face_len - column :], core_high[face_len - column :]], axis=0
            ),
        ]
    )
    slab_recv = extended(slab_send, ((SLAB, 0),), 1)
    low_full = slab_recv[0]
    high_full = slab_recv[3]
    slab_low = low_full[:face_len]
    slab_high = high_full[:face_len]
    tile_low = jnp.concatenate(
        [low_full[face_len : face_len + column], core_low, high_full[face_len : face_len + column]],
        axis=0,
    )
    tile_high = jnp.concatenate(
        [low_full[face_len + column :], core_high, high_full[face_len + column :]], axis=0
    )
    zero_row = jnp.zeros((1, local_rows.shape[1]), local_rows.dtype)
    return jnp.concatenate([local_rows, slab_low, slab_high, tile_low, tile_high, zero_row], axis=0)


def pick_rows(lookup, tap_index, offset, block_rows, flat_weight):
    gathered = jnp.take(lookup, tap_index.T, axis=0)
    gathered = gathered.reshape(block_rows, tap_index.shape[0] * lookup.shape[1])
    return jnp.dot(gathered, flat_weight, preferred_element_type=jnp.float32)


def convolve(lookup, tap_index, weight):
    total_rows = tap_index.shape[1]
    block_rows = min(512, total_rows)
    flat_weight = weight.reshape(weight.shape[0] * weight.shape[1], weight.shape[2])
    compute = partial(pick_rows, lookup, tap_index, 0, block_rows, flat_weight)
    result = compute()
    return result


def normalize(conv_out, live_mask, count_value, gain, shift):
    first_sum = jnp.sum(conv_out * live_mask, axis=0)
    square_sum = jnp.sum(conv_out * conv_out * live_mask, axis=0)
    channel_sums, square_sums, voxel_total = (
        by_axis(first_sum, SLAB_TILE),
        by_axis(square_sum, SLAB_TILE),
        by_axis(count_value, SLAB_TILE),
    )
    average = channel_sums / voxel_total
    variance = square_sums / voxel_total - average * average
    return (conv_out - average) * lax.rsqrt(variance + EPSILON) * gain + shift


def per_device(
    features,
    counts,
    rulebook,
    face_rows,
    conv_one,
    gain_one,
    shift_one,
    conv_two,
    gain_two,
    shift_two,
):
    local_rows = features[0, 0]
    face_lists = face_rows[0, 0]
    tap_index = rulebook[0, 0]
    voxel_count = counts[0, 0]
    count_value = voxel_count.astype(jnp.float32)
    live_mask = (lax.broadcasted_iota(jnp.int32, (local_rows.shape[0], 1), 0) < voxel_count).astype(
        jnp.float32
    )
    first = convolve(build_table(local_rows, face_lists), tap_index, conv_one)
    hidden = (
        live_mask * jnp.maximum(normalize(first, live_mask, count_value, gain_one, shift_one), 0.0)
    ).astype(jnp.bfloat16)
    second = convolve(build_table(hidden, face_lists), tap_index, conv_two)
    summed = normalize(second, live_mask, count_value, gain_two, shift_two) + local_rows.astype(
        jnp.float32
    )
    output = (live_mask * jnp.maximum(summed, 0.0)).astype(jnp.bfloat16)
    return output[None, None]


def solution(mesh):
    torus = Mesh(
        mesh.devices.reshape(8, 4, 2, mesh.shape["tile"]), ("slab_0", "slab_1", "slab_2", "tile")
    )
    in_specs = (
        P(SLAB, "tile", None, None),
        P(SLAB, "tile"),
        P(SLAB, "tile", None, None),
        P(SLAB, "tile", None, None),
        P(),
        P(),
        P(),
        P(),
        P(),
        P(),
    )
    out_specs = P(SLAB, "tile", None, None)
    return jax.shard_map(
        per_device, mesh=torus, in_specs=in_specs, out_specs=out_specs, check_vma=False
    )
```

profile of v0, /device:TPU:2, one launch (start us, length us, event | category | flops | bytes accessed | tf_op | source)
XLA Modules:
  0.0 231.2 jit_solution(8170010614980495106)
XLA Ops:
  0.9 1.6 gather_fusion
  2.5 3.5 %collective-permute-start = (bf16[1,64,128]{2,1,0:T(8,128)(2,1)S(1)}, bf16[1,64,128]{2,1,0:T(8,128)(2,1)S(1)}, u32[]{:S(2)}, u32[]{:S(2)}) collective-permute-start(bf16[1,64,128]{2,1,0:T(8,128)(2,1)S(1)} %get-tuple-element.42), channel_id=1, source_target_pairs={{0,1},{1,2},{2,3},{3,4},{4,5},{5,6},{6,7},{8,9},{9,10},{10,11},{11... | collective-permute-start | bytes 49160 | tf_op jit(solution)/shard_map/ppermute | solution.py:19
  11.6 1.9 collective-permute-start.2
  13.6 3.6 %collective-permute-start.3 = (bf16[1,80,128]{2,1,0:T(8,128)(2,1)S(1)}, bf16[1,80,128]{2,1,0:T(8,128)(2,1)S(1)}, u32[]{:S(2)}, u32[]{:S(2)}) collective-permute-start(bf16[1,80,128]{2,1,0:T(8,128)(2,1)S(1)} %maximum_bitcast_fusion.1), channel_id=1, source_target_pairs={{8,0},{16,8},{24,16},{32,24},{40,32},{48,40},{56,48},{64,56},{72,6... | collective-permute-start | bytes 61448 | tf_op jit(solution)/shard_map/ppermute | solution.py:22
  17.2 1.4 collective-permute-done.3
  18.8 28.4 %gather_fusion.2 = bf16[13824,128]{1,0:T(8,128)(2,1)} fusion(bf16[801,128]{1,0:T(8,128)(2,1)S(1)} %constant_dynamic-update-slice_fusion, s32[14336]{0:T(1024)S(1)} %pad_clamp_fusion), kind=kCustom, calls=%fused_computation.clone | custom fusion | bytes 7133184 | tf_op jit(solution)/shard_map/jit(_take)/gather | solution.py:65
  47.1 6.6 %reshape.125 = bf16[512,27,128]{2,1,0:T(8,128)(2,1)} reshape(bf16[13824,128]{1,0:T(8,128)(2,1)} %gather_fusion.2) | data formatting | bytes 7077888 | tf_op jit(solution)/shard_map/jit(_take)/gather | solution.py:65
  53.7 10.1 %broadcast_select_fusion = bf16[512,27,128]{2,1,0:T(8,128)(2,1)S(1)} fusion(bf16[512,27,128]{2,1,0:T(8,128)(2,1)} %reshape.125, pred[512,27]{1,0:T(8,128)(4,1)S(1)} %copy.13), kind=kLoop, calls=%fused_computation.4 | loop fusion | flops 1769472 | bytes 7091712 | tf_op jit(solution)/shard_map/jit(_take)/select_n | solution.py:65
  65.1 23.7 %all-reduce.3 = (f32[128]{0:T(128)S(1)}, f32[]{:T(128)}, f32[128]{0:T(128)S(1)}) all-reduce(f32[128]{0:T(128)S(1)} %get-tuple-element.9, f32[]{:T(128)S(6)} %convert_element_type.21, f32[128]{0:T(128)S(1)} %get-tuple-element.8), channel_id=1, replica_groups=mesh['slab_0'=8,'slab_1'=4,'slab_2'=2,'tile'=8] {'slab_0'}, use_global_device_ids=true, to_apply=%region_1.3 | all-reduce | flops 257 | bytes 2056 | tf_op jit(solution)/shard_map/psum | solution.py:29
  88.8 11.0 %all-reduce.5 = (f32[128]{0:T(128)S(1)}, f32[]{:T(128)}, f32[128]{0:T(128)S(1)}) all-reduce(f32[128]{0:T(128)S(1)} %get-tuple-element.17, f32[]{:T(128)} %get-tuple-element.18, f32[128]{0:T(128)S(1)} %get-tuple-element.19), channel_id=1, replica_groups=mesh['slab_0'=8,'slab_1'=4,'slab_2'=2,'tile'=8] {'slab_1'}, use_global_device_ids=true, to_apply=%region_2.4 | all-reduce | flops 257 | bytes 2056 | tf_op jit(solution)/shard_map/psum | solution.py:29
  99.8 3.1 %all-reduce.7 = (f32[128]{0:T(128)S(1)}, f32[]{:T(128)}, f32[128]{0:T(128)S(1)}) all-reduce(f32[128]{0:T(128)S(1)} %get-tuple-element.22, f32[]{:T(128)} %get-tuple-element.23, f32[128]{0:T(128)S(1)} %get-tuple-element.24), channel_id=1, replica_groups=mesh['slab_0'=8,'slab_1'=4,'slab_2'=2,'tile'=8] {'slab_2'}, use_global_device_ids=true, to_apply=%region_3.5 | all-reduce | flops 257 | bytes 2056 | tf_op jit(solution)/shard_map/psum | solution.py:29
  102.9 18.8 %all-reduce.1 = (f32[128]{0:T(128)S(1)}, f32[]{:T(128)}, f32[128]{0:T(128)S(1)}) all-reduce(f32[128]{0:T(128)S(1)} %get-tuple-element.27, f32[]{:T(128)} %get-tuple-element.28, f32[128]{0:T(128)S(1)} %get-tuple-element.29), channel_id=1, replica_groups=mesh['slab_0'=8,'slab_1'=4,'slab_2'=2,'tile'=8] {'tile'}, use_global_device_ids=true, to_apply=%region_4.6 | all-reduce | flops 257 | bytes 2056 | tf_op jit(solution)/shard_map/psum | solution.py:29
  123.4 2.7 %collective-permute-start.4 = (bf16[1,64,128]{2,1,0:T(8,128)(2,1)S(1)}, bf16[1,64,128]{2,1,0:T(8,128)(2,1)S(1)}, u32[]{:S(2)}, u32[]{:S(2)}) collective-permute-start(bf16[1,64,128]{2,1,0:T(8,128)(2,1)S(1)} %get-tuple-element.38), channel_id=1, source_target_pairs={{0,1},{1,2},{2,3},{3,4},{4,5},{5,6},{6,7},{8,9},{9,10},{10,11},{11... | collective-permute-start | bytes 49160 | tf_op jit(solution)/shard_map/ppermute | solution.py:19
  127.6 4.2 %collective-permute-done.5 = bf16[1,64,128]{2,1,0:T(8,128)(2,1)S(1)} collective-permute-done((bf16[1,64,128]{2,1,0:T(8,128)(2,1)S(1)}, bf16[1,64,128]{2,1,0:T(8,128)(2,1)S(1)}, u32[]{:S(2)}, u32[]{:S(2)}) %collective-permute-start.5) | collective-permute-done | bytes 16416 | tf_op jit(solution)/shard_map/ppermute | solution.py:22
  131.8 1.9 collective-permute-start.6
  133.7 3.6 %collective-permute-start.7 = (bf16[1,80,128]{2,1,0:T(8,128)(2,1)S(1)}, bf16[1,80,128]{2,1,0:T(8,128)(2,1)S(1)}, u32[]{:S(2)}, u32[]{:S(2)}) collective-permute-start(bf16[1,80,128]{2,1,0:T(8,128)(2,1)S(1)} %maximum_bitcast_fusion.3), channel_id=1, source_target_pairs={{8,0},{16,8},{24,16},{32,24},{40,32},{48,40},{56,48},{64,56},{72,6... | collective-permute-start | bytes 61448 | tf_op jit(solution)/shard_map/ppermute | solution.py:22
  137.4 1.4 collective-permute-done.7
  138.9 28.4 %gather_fusion.3 = bf16[13824,128]{1,0:T(8,128)(2,1)} fusion(bf16[801,128]{1,0:T(8,128)(2,1)S(1)} %constant_dynamic-update-slice_fusion.10, s32[14336]{0:T(1024)S(1)} %pad_clamp_fusion), kind=kCustom, calls=%fused_computation.1.clone | custom fusion | bytes 7133184 | tf_op jit(solution)/shard_map/jit(_take)/gather | solution.py:65
  167.3 6.6 %reshape.129 = bf16[512,27,128]{2,1,0:T(8,128)(2,1)} reshape(bf16[13824,128]{1,0:T(8,128)(2,1)} %gather_fusion.3) | data formatting | bytes 7077888 | tf_op jit(solution)/shard_map/jit(_take)/gather | solution.py:65
  173.9 10.1 %broadcast_select_fusion.1 = bf16[512,27,128]{2,1,0:T(8,128)(2,1)S(1)} fusion(bf16[512,27,128]{2,1,0:T(8,128)(2,1)} %reshape.129, pred[512,27]{1,0:T(8,128)(4,1)S(1)} %copy.13), kind=kLoop, calls=%fused_computation.5 | loop fusion | flops 1769472 | bytes 7091712 | tf_op jit(solution)/shard_map/jit(_take)/select_n | solution.py:65
  185.3 14.2 %all-reduce.2 = (f32[128]{0:T(128)S(1)}, f32[128]{0:T(128)S(1)}) all-reduce(f32[128]{0:T(128)S(1)} %get-tuple-element.7, f32[128]{0:T(128)S(1)} %get-tuple-element.6), channel_id=1, replica_groups=mesh['slab_0'=8,'slab_1'=4,'slab_2'=2,'tile'=8] {'slab_0'}, use_global_device_ids=true, to_apply=%region_15.17 | all-reduce | flops 256 | bytes 2048 | tf_op jit(solution)/shard_map/psum | solution.py:29
  199.5 10.2 %all-reduce.4 = (f32[128]{0:T(128)S(1)}, f32[128]{0:T(128)S(1)}) all-reduce(f32[128]{0:T(128)S(1)} %get-tuple-element.15, f32[128]{0:T(128)S(1)} %get-tuple-element.16), channel_id=1, replica_groups=mesh['slab_0'=8,'slab_1'=4,'slab_2'=2,'tile'=8] {'slab_1'}, use_global_device_ids=true, to_apply=%region_16.18 | all-reduce | flops 256 | bytes 2048 | tf_op jit(solution)/shard_map/psum | solution.py:29
  209.7 2.5 %all-reduce.6 = (f32[128]{0:T(128)S(1)}, f32[128]{0:T(128)S(1)}) all-reduce(f32[128]{0:T(128)S(1)} %get-tuple-element.20, f32[128]{0:T(128)S(1)} %get-tuple-element.21), channel_id=1, replica_groups=mesh['slab_0'=8,'slab_1'=4,'slab_2'=2,'tile'=8] {'slab_2'}, use_global_device_ids=true, to_apply=%region_17.19 | all-reduce | flops 256 | bytes 2048 | tf_op jit(solution)/shard_map/psum | solution.py:29
  212.2 17.6 %all-reduce = (f32[128]{0:T(128)S(1)}, f32[128]{0:T(128)S(1)}) all-reduce(f32[128]{0:T(128)S(1)} %get-tuple-element.25, f32[128]{0:T(128)S(1)} %get-tuple-element.26), channel_id=1, replica_groups=mesh['slab_0'=8,'slab_1'=4,'slab_2'=2,'tile'=8] {'tile'}, use_global_device_ids=true, to_apply=%region_18.20 | all-reduce | flops 256 | bytes 2048 | tf_op jit(solution)/shard_map/psum | solution.py:29
  (67 shorter events, 13.1 us)
Async XLA Ops:
  0.0 63.8 %copy-start = (bf16[27,128,128]{2,1,0:T(8,128)(2,1)S(1)}, bf16[27,128,128]{2,1,0:T(8,128)(2,1)}, u32[]{:S(2)}) copy-start(bf16[27,128,128]{2,1,0:T(8,128)(2,1)} %param.16) | copy-start | bytes 2654212
  2.5 8.6 %collective-permute-start = (bf16[1,64,128]{2,1,0:T(8,128)(2,1)S(1)}, bf16[1,64,128]{2,1,0:T(8,128)(2,1)S(1)}, u32[]{:S(2)}, u32[]{:S(2)}) collective-permute-start(bf16[1,64,128]{2,1,0:T(8,128)(2,1)S(1)} %get-tuple-element.42), channel_id=1, source_target_pairs={{0,1},{1,2},{2,3},{3,4},{4,5},{5,6},{6,7},{8,9},{9,10},{10,11},{11... | collective-permute-start | bytes 49160 | tf_op jit(solution)/shard_map/ppermute | solution.py:19
  6.0 5.6 %collective-permute-start.1 = (bf16[1,64,128]{2,1,0:T(8,128)(2,1)S(1)}, bf16[1,64,128]{2,1,0:T(8,128)(2,1)S(1)}, u32[]{:S(2)}, u32[]{:S(2)}) collective-permute-start(bf16[1,64,128]{2,1,0:T(8,128)(2,1)S(1)} %get-tuple-element.41), channel_id=1, source_target_pairs={{1,0},{2,1},{3,2},{4,3},{5,4},{6,5},{7,6},{9,8},{10,9},{11,10},{12... | collective-permute-start | bytes 49160 | tf_op jit(solution)/shard_map/ppermute | solution.py:22
  11.6 5.6 %collective-permute-start.2 = (bf16[1,80,128]{2,1,0:T(8,128)(2,1)S(1)}, bf16[1,80,128]{2,1,0:T(8,128)(2,1)S(1)}, u32[]{:S(2)}, u32[]{:S(2)}) collective-permute-start(bf16[1,80,128]{2,1,0:T(8,128)(2,1)S(1)} %maximum_bitcast_fusion), channel_id=1, source_target_pairs={{0,8},{8,16},{16,24},{24,32},{32,40},{40,48},{48,56},{56,64},{64,7... | collective-permute-start | bytes 61448 | tf_op jit(solution)/shard_map/ppermute | solution.py:19
  13.6 5.1 %collective-permute-start.3 = (bf16[1,80,128]{2,1,0:T(8,128)(2,1)S(1)}, bf16[1,80,128]{2,1,0:T(8,128)(2,1)S(1)}, u32[]{:S(2)}, u32[]{:S(2)}) collective-permute-start(bf16[1,80,128]{2,1,0:T(8,128)(2,1)S(1)} %maximum_bitcast_fusion.1), channel_id=1, source_target_pairs={{8,0},{16,8},{24,16},{32,24},{40,32},{48,40},{56,48},{64,56},{72,6... | collective-permute-start | bytes 61448 | tf_op jit(solution)/shard_map/ppermute | solution.py:22
  63.8 58.6 %copy-start.2 = (f32[128]{0:T(128)S(1)}, f32[128]{0:T(128)}, u32[]{:S(2)}) copy-start(f32[128]{0:T(128)} %param.18) | copy-start | bytes 1540
  63.8 58.6 %copy-start.3 = (f32[128]{0:T(128)S(1)}, f32[128]{0:T(128)}, u32[]{:S(2)}) copy-start(f32[128]{0:T(128)} %param.17) | copy-start | bytes 1540
  123.4 4.2 %collective-permute-start.4 = (bf16[1,64,128]{2,1,0:T(8,128)(2,1)S(1)}, bf16[1,64,128]{2,1,0:T(8,128)(2,1)S(1)}, u32[]{:S(2)}, u32[]{:S(2)}) collective-permute-start(bf16[1,64,128]{2,1,0:T(8,128)(2,1)S(1)} %get-tuple-element.38), channel_id=1, source_target_pairs={{0,1},{1,2},{2,3},{3,4},{4,5},{5,6},{6,7},{8,9},{9,10},{10,11},{11... | collective-permute-start | bytes 49160 | tf_op jit(solution)/shard_map/ppermute | solution.py:19
  126.2 5.6 %collective-permute-start.5 = (bf16[1,64,128]{2,1,0:T(8,128)(2,1)S(1)}, bf16[1,64,128]{2,1,0:T(8,128)(2,1)S(1)}, u32[]{:S(2)}, u32[]{:S(2)}) collective-permute-start(bf16[1,64,128]{2,1,0:T(8,128)(2,1)S(1)} %get-tuple-element.37), channel_id=1, source_target_pairs={{1,0},{2,1},{3,2},{4,3},{5,4},{6,5},{7,6},{9,8},{10,9},{11,10},{12... | collective-permute-start | bytes 49160 | tf_op jit(solution)/shard_map/ppermute | solution.py:22
  131.8 5.6 %collective-permute-start.6 = (bf16[1,80,128]{2,1,0:T(8,128)(2,1)S(1)}, bf16[1,80,128]{2,1,0:T(8,128)(2,1)S(1)}, u32[]{:S(2)}, u32[]{:S(2)}) collective-permute-start(bf16[1,80,128]{2,1,0:T(8,128)(2,1)S(1)} %maximum_bitcast_fusion.2), channel_id=1, source_target_pairs={{0,8},{8,16},{16,24},{24,32},{32,40},{40,48},{48,56},{56,64},{64,7... | collective-permute-start | bytes 61448 | tf_op jit(solution)/shard_map/ppermute | solution.py:19
  133.7 5.1 %collective-permute-start.7 = (bf16[1,80,128]{2,1,0:T(8,128)(2,1)S(1)}, bf16[1,80,128]{2,1,0:T(8,128)(2,1)S(1)}, u32[]{:S(2)}, u32[]{:S(2)}) collective-permute-start(bf16[1,80,128]{2,1,0:T(8,128)(2,1)S(1)} %maximum_bitcast_fusion.3), channel_id=1, source_target_pairs={{8,0},{16,8},{24,16},{32,24},{40,32},{48,40},{56,48},{64,56},{72,6... | collective-permute-start | bytes 61448 | tf_op jit(solution)/shard_map/ppermute | solution.py:22
  173.9 10.2 %copy-start.6 = (bf16[27,128,128]{2,1,0:T(8,128)(2,1)S(1)}, bf16[27,128,128]{2,1,0:T(8,128)(2,1)}, u32[]{:S(2)}) copy-start(bf16[27,128,128]{2,1,0:T(8,128)(2,1)} %param.19) | copy-start | bytes 2654212
  184.1 46.4 %copy-start.1 = (bf16[1,1,512,128]{3,2,1,0:T(8,128)(2,1)S(1)}, bf16[1,1,512,128]{3,2,1,0:T(8,128)(2,1)}, u32[]{:S(2)}) copy-start(bf16[1,1,512,128]{3,2,1,0:T(8,128)(2,1)} %param.12) | copy-start | bytes 393220
  184.1 46.4 %copy-start.4 = (f32[128]{0:T(128)S(1)}, f32[128]{0:T(128)}, u32[]{:S(2)}) copy-start(f32[128]{0:T(128)} %param.21) | copy-start | bytes 1540
  184.1 46.4 %copy-start.5 = (f32[128]{0:T(128)S(1)}, f32[128]{0:T(128)}, u32[]{:S(2)}) copy-start(f32[128]{0:T(128)} %param.20) | copy-start | bytes 1540
where the time goes:
time: 233 us; the launch traced here: 231 us
  blocking collectives  101 us (43%)
  local copies, waits for them, and re-layouts  74.2 us (32%)
  other arithmetic  24.9 us (11%)
  starting transfers between devices  19.9 us (9%)
  waiting for transfers between devices  7.7 us (3%)
  matrix products  2.55 us (1%)
    psum x8, blocking collectives, by_axis(): shard = lax.psum(shard, axis)  101 us
    gather x4, local copies, waits for them, and re-layouts, pick_rows(): gathered = jnp.take(lookup, tap_index.T, axis=0)  69.9 us
    select_n x3, other arithmetic, pick_rows(): gathered = jnp.take(lookup, tap_index.T, axis=0)  21 us
    ppermute x4, starting transfers between devices, extended(): lax.ppermute(lax.slice_in_dim(block, block.shape[dim] - width, None, axis...  10 us
    ppermute x4, starting transfers between devices, extended(): lax.ppermute(lax.slice_in_dim(block, 0, width, axis=dim), axis, backward)  9.87 us
    ppermute x4, waiting for transfers between devices, extended(): lax.ppermute(lax.slice_in_dim(block, 0, width, axis=dim), axis, backward)  7.57 us
  transfers between devices with their start and end apart: 8, of which 5 were waited for; matrix products, arithmetic and copies ran while one was open for 1% of the time, Pallas kernels for 0%

commit v1 on v0

--- a/solution.py
+++ b/solution.py
@@ -26,7 +26,7 @@
 
 def by_axis(shard, axes):
     for axis in axes:
-        shard = lax.psum(shard, axis)
+        shard = jnp.sum(lax.all_gather(shard, axis), axis=0)
     return shard
 
 

time: 233 us -> 358 us (1.54)
  the two profiles are of different devices: /device:TPU:2 before, /device:TPU:24 now
where the time goes in v1:
time: 358 us; the launch traced here: 356 us
  blocking collectives  215 us (60%)
  local copies, waits for them, and re-layouts  84 us (23%)
  other arithmetic  27.9 us (8%)
  starting transfers between devices  17.6 us (5%)
  waiting for transfers between devices  7.89 us (2%)
    all_gather x16, blocking collectives, by_axis(): shard = jnp.sum(lax.all_gather(shard, axis), axis=0)  163 us
    gather x4, local copies, waits for them, and re-layouts, pick_rows(): gathered = jnp.take(lookup, tap_index.T, axis=0)  69.9 us
    unnamed x4, blocking collectives  52.2 us
    select_n x3, other arithmetic, pick_rows(): gathered = jnp.take(lookup, tap_index.T, axis=0)  21 us
    unnamed x43, local copies, waits for them, and re-layouts  10.9 us
    ppermute x4, starting transfers between devices, extended(): lax.ppermute(lax.slice_in_dim(block, block.shape[dim] - width, None, axis...  10.4 us
    ppermute x4, waiting for transfers between devices, extended(): lax.ppermute(lax.slice_in_dim(block, 0, width, axis=dim), axis, backward)  7.88 us
    ppermute x4, starting transfers between devices, extended(): lax.ppermute(lax.slice_in_dim(block, 0, width, axis=dim), axis, backward)  7.21 us
  transfers between devices with their start and end apart: 8, of which 3 were waited for; matrix products, arithmetic and copies ran while one was open for 4% of the time, Pallas kernels for 0%

profile of v1, /device:TPU:24, one launch (start us, length us, event | category | flops | bytes accessed | tf_op | source)
XLA Modules:
  0.0 356.2 jit_solution(18365566848309902229)
XLA Ops:
  2.5 4.7 %collective-permute-start = (bf16[1,64,128]{2,1,0:T(8,128)(2,1)S(1)}, bf16[1,64,128]{2,1,0:T(8,128)(2,1)S(1)}, u32[]{:S(2)}, u32[]{:S(2)}) collective-permute-start(bf16[1,64,128]{2,1,0:T(8,128)(2,1)S(1)} %get-tuple-element.22), channel_id=1, source_target_pairs={{0,1},{1,2},{2,3},{3,4},{4,5},{5,6},{6,7},{8,9},{9,10},{10,11},{11... | collective-permute-start | bytes 49160 | tf_op jit(solution)/shard_map/ppermute | solution.py:19
  14.7 23.2 %all-reduce = f32[8]{0:T(128)S(1)} all-reduce(f32[8]{0:T(128)S(1)} %dynamic-update-slice), channel_id=1, replica_groups=mesh['slab_0'=8,'slab_1'=4,'slab_2'=2,'tile'=8] {'slab_0'}, use_global_device_ids=true, to_apply=%add | all-reduce | flops 8 | bytes 64
  41.2 10.5 %all-reduce.1 = f32[4]{0:T(128)S(1)} all-reduce(f32[4]{0:T(128)S(1)} %dynamic-update-slice.1), channel_id=1, replica_groups=mesh['slab_0'=8,'slab_1'=4,'slab_2'=2,'tile'=8] {'slab_1'}, use_global_device_ids=true, to_apply=%add.1 | all-reduce | flops 4 | bytes 32
  60.7 16.1 %all-reduce.3 = f32[8]{0:T(128)S(1)} all-reduce(f32[8]{0:T(128)S(1)} %dynamic-update-slice.3), channel_id=1, replica_groups=mesh['slab_0'=8,'slab_1'=4,'slab_2'=2,'tile'=8] {'tile'}, use_global_device_ids=true, to_apply=%add.3 | all-reduce | flops 8 | bytes 64
  82.1 28.4 %gather_fusion.2 = bf16[13824,128]{1,0:T(8,128)(2,1)} fusion(bf16[801,128]{1,0:T(8,128)(2,1)S(1)} %constant_dynamic-update-slice_fusion, s32[14336]{0:T(1024)S(1)} %pad_clamp_fusion), kind=kCustom, calls=%fused_computation.clone | custom fusion | bytes 7133184 | tf_op jit(solution)/shard_map/jit(_take)/gather | solution.py:65
  110.5 6.6 %reshape.229 = bf16[512,27,128]{2,1,0:T(8,128)(2,1)} reshape(bf16[13824,128]{1,0:T(8,128)(2,1)} %gather_fusion.2) | data formatting | bytes 7077888 | tf_op jit(solution)/shard_map/jit(_take)/gather | solution.py:65
  117.1 10.1 %broadcast_select_fusion = bf16[512,27,128]{2,1,0:T(8,128)(2,1)S(1)} fusion(bf16[512,27,128]{2,1,0:T(8,128)(2,1)} %reshape.229, pred[512,27]{1,0:T(8,128)(4,1)S(1)} %copy.19), kind=kLoop, calls=%fused_computation.4 | loop fusion | flops 1769472 | bytes 7091712 | tf_op jit(solution)/shard_map/jit(_take)/select_n | solution.py:65
  128.5 17.8 %all-gather.16 = f32[8,1,128]{2,1,0:T(1,128)S(1)} all-gather(f32[1,1,128]{2,1,0:T(1,128)S(1)} %bitcast.147), channel_id=2, replica_groups=mesh['slab_0'=8,'slab_1'=4,'slab_2'=2,'tile'=8] {'slab_0'}, dimensions={0}, use_global_device_ids=true | all-gather | bytes 4608 | tf_op jit(solution)/shard_map/all_gather | solution.py:29
  146.3 7.0 %all-gather.17 = f32[4,1,128]{2,1,0:T(1,128)S(1)} all-gather(f32[1,1,128]{2,1,0:T(1,128)S(1)} %bitcast.137), channel_id=3, replica_groups=mesh['slab_0'=8,'slab_1'=4,'slab_2'=2,'tile'=8] {'slab_1'}, dimensions={0}, use_global_device_ids=true | all-gather | bytes 2560 | tf_op jit(solution)/shard_map/all_gather | solution.py:29
  155.1 13.3 %all-gather.19 = f32[8,1,128]{2,1,0:T(1,128)S(1)} all-gather(f32[1,1,128]{2,1,0:T(1,128)S(1)} %bitcast.141), channel_id=5, replica_groups=mesh['slab_0'=8,'slab_1'=4,'slab_2'=2,'tile'=8] {'tile'}, dimensions={0}, use_global_device_ids=true | all-gather | bytes 4608 | tf_op jit(solution)/shard_map/all_gather | solution.py:29
  168.4 14.6 %all-gather.20 = f32[8,1,128]{2,1,0:T(1,128)S(1)} all-gather(f32[1,1,128]{2,1,0:T(1,128)S(1)} %bitcast.145), channel_id=6, replica_groups=mesh['slab_0'=8,'slab_1'=4,'slab_2'=2,'tile'=8] {'slab_0'}, dimensions={0}, use_global_device_ids=true | all-gather | bytes 4608 | tf_op jit(solution)/shard_map/all_gather | solution.py:29
  183.1 9.0 %all-gather.21 = f32[4,1,128]{2,1,0:T(1,128)S(1)} all-gather(f32[1,1,128]{2,1,0:T(1,128)S(1)} %bitcast.138), channel_id=7, replica_groups=mesh['slab_0'=8,'slab_1'=4,'slab_2'=2,'tile'=8] {'slab_1'}, dimensions={0}, use_global_device_ids=true | all-gather | bytes 2560 | tf_op jit(solution)/shard_map/all_gather | solution.py:29
  193.9 15.3 %all-gather.23 = f32[8,1,128]{2,1,0:T(1,128)S(1)} all-gather(f32[1,1,128]{2,1,0:T(1,128)S(1)} %bitcast.142), channel_id=9, replica_groups=mesh['slab_0'=8,'slab_1'=4,'slab_2'=2,'tile'=8] {'tile'}, dimensions={0}, use_global_device_ids=true | all-gather | bytes 4608 | tf_op jit(solution)/shard_map/all_gather | solution.py:29
  211.0 3.1 collective-permute-start.4
  216.8 4.1 %collective-permute-done.5 = bf16[1,64,128]{2,1,0:T(8,128)(2,1)S(1)} collective-permute-done((bf16[1,64,128]{2,1,0:T(8,128)(2,1)S(1)}, bf16[1,64,128]{2,1,0:T(8,128)(2,1)S(1)}, u32[]{:S(2)}, u32[]{:S(2)}) %collective-permute-start.5) | collective-permute-done | bytes 16416 | tf_op jit(solution)/shard_map/ppermute | solution.py:22
  225.7 28.4 %gather_fusion.3 = bf16[13824,128]{1,0:T(8,128)(2,1)} fusion(bf16[801,128]{1,0:T(8,128)(2,1)S(1)} %constant_dynamic-update-slice_fusion.10, s32[14336]{0:T(1024)S(1)} %pad_clamp_fusion), kind=kCustom, calls=%fused_computation.1.clone | custom fusion | bytes 7133184 | tf_op jit(solution)/shard_map/jit(_take)/gather | solution.py:65
  254.0 6.6 %reshape.233 = bf16[512,27,128]{2,1,0:T(8,128)(2,1)} reshape(bf16[13824,128]{1,0:T(8,128)(2,1)} %gather_fusion.3) | data formatting | bytes 7077888 | tf_op jit(solution)/shard_map/jit(_take)/gather | solution.py:65
  260.6 10.1 %broadcast_select_fusion.1 = bf16[512,27,128]{2,1,0:T(8,128)(2,1)S(1)} fusion(bf16[512,27,128]{2,1,0:T(8,128)(2,1)} %reshape.233, pred[512,27]{1,0:T(8,128)(4,1)S(1)} %copy.19), kind=kLoop, calls=%fused_computation.5 | loop fusion | flops 1769472 | bytes 7091712 | tf_op jit(solution)/shard_map/jit(_take)/select_n | solution.py:65
  272.1 18.5 %all-gather.24 = f32[8,1,128]{2,1,0:T(1,128)S(1)} all-gather(f32[1,1,128]{2,1,0:T(1,128)S(1)} %bitcast.148), channel_id=10, replica_groups=mesh['slab_0'=8,'slab_1'=4,'slab_2'=2,'tile'=8] {'slab_0'}, dimensions={0}, use_global_device_ids=true | all-gather | bytes 4608 | tf_op jit(solution)/shard_map/all_gather | solution.py:29
  290.6 7.0 %all-gather.25 = f32[4,1,128]{2,1,0:T(1,128)S(1)} all-gather(f32[1,1,128]{2,1,0:T(1,128)S(1)} %bitcast.139), channel_id=11, replica_groups=mesh['slab_0'=8,'slab_1'=4,'slab_2'=2,'tile'=8] {'slab_1'}, dimensions={0}, use_global_device_ids=true | all-gather | bytes 2560 | tf_op jit(solution)/shard_map/all_gather | solution.py:29
  299.4 13.0 %all-gather.27 = f32[8,1,128]{2,1,0:T(1,128)S(1)} all-gather(f32[1,1,128]{2,1,0:T(1,128)S(1)} %bitcast.143), channel_id=13, replica_groups=mesh['slab_0'=8,'slab_1'=4,'slab_2'=2,'tile'=8] {'tile'}, dimensions={0}, use_global_device_ids=true | all-gather | bytes 4608 | tf_op jit(solution)/shard_map/all_gather | solution.py:29
  312.4 15.9 %all-gather.28 = f32[8,1,128]{2,1,0:T(1,128)S(1)} all-gather(f32[1,1,128]{2,1,0:T(1,128)S(1)} %bitcast.146), channel_id=14, replica_groups=mesh['slab_0'=8,'slab_1'=4,'slab_2'=2,'tile'=8] {'slab_0'}, dimensions={0}, use_global_device_ids=true | all-gather | bytes 4608 | tf_op jit(solution)/shard_map/all_gather | solution.py:29
  328.3 9.0 %all-gather.29 = f32[4,1,128]{2,1,0:T(1,128)S(1)} all-gather(f32[1,1,128]{2,1,0:T(1,128)S(1)} %bitcast.140), channel_id=15, replica_groups=mesh['slab_0'=8,'slab_1'=4,'slab_2'=2,'tile'=8] {'slab_1'}, dimensions={0}, use_global_device_ids=true | all-gather | bytes 2560 | tf_op jit(solution)/shard_map/all_gather | solution.py:29
  339.1 15.6 %all-gather.31 = f32[8,1,128]{2,1,0:T(1,128)S(1)} all-gather(f32[1,1,128]{2,1,0:T(1,128)S(1)} %bitcast.144), channel_id=17, replica_groups=mesh['slab_0'=8,'slab_1'=4,'slab_2'=2,'tile'=8] {'tile'}, dimensions={0}, use_global_device_ids=true | all-gather | bytes 4608 | tf_op jit(solution)/shard_map/all_gather | solution.py:29
  (111 shorter events, 47.5 us)
Async XLA Ops:
  0.0 127.2 %copy-start = (bf16[27,128,128]{2,1,0:T(8,128)(2,1)S(1)}, bf16[27,128,128]{2,1,0:T(8,128)(2,1)}, u32[]{:S(2)}) copy-start(bf16[27,128,128]{2,1,0:T(8,128)(2,1)} %param.16) | copy-start | bytes 2654212
  2.5 75.1 %collective-permute-start = (bf16[1,64,128]{2,1,0:T(8,128)(2,1)S(1)}, bf16[1,64,128]{2,1,0:T(8,128)(2,1)S(1)}, u32[]{:S(2)}, u32[]{:S(2)}) collective-permute-start(bf16[1,64,128]{2,1,0:T(8,128)(2,1)S(1)} %get-tuple-element.22), channel_id=1, source_target_pairs={{0,1},{1,2},{2,3},{3,4},{4,5},{5,6},{6,7},{8,9},{9,10},{10,11},{11... | collective-permute-start | bytes 49160 | tf_op jit(solution)/shard_map/ppermute | solution.py:19
  7.2 70.4 %collective-permute-start.1 = (bf16[1,64,128]{2,1,0:T(8,128)(2,1)S(1)}, bf16[1,64,128]{2,1,0:T(8,128)(2,1)S(1)}, u32[]{:S(2)}, u32[]{:S(2)}) collective-permute-start(bf16[1,64,128]{2,1,0:T(8,128)(2,1)S(1)} %get-tuple-element.21), channel_id=1, source_target_pairs={{1,0},{2,1},{3,2},{4,3},{5,4},{6,5},{7,6},{9,8},{10,9},{11,10},{12... | collective-permute-start | bytes 49160 | tf_op jit(solution)/shard_map/ppermute | solution.py:22
  77.6 2.6 collective-permute-start.2
  79.0 3.1 collective-permute-start.3
  127.2 82.8 %copy-start.2 = (f32[128]{0:T(128)S(1)}, f32[128]{0:T(128)}, u32[]{:S(2)}) copy-start(f32[128]{0:T(128)} %param.18) | copy-start | bytes 1540
  127.2 82.8 %copy-start.3 = (f32[128]{0:T(128)S(1)}, f32[128]{0:T(128)}, u32[]{:S(2)}) copy-start(f32[128]{0:T(128)} %param.17) | copy-start | bytes 1540
  211.0 5.9 %collective-permute-start.4 = (bf16[1,64,128]{2,1,0:T(8,128)(2,1)S(1)}, bf16[1,64,128]{2,1,0:T(8,128)(2,1)S(1)}, u32[]{:S(2)}, u32[]{:S(2)}) collective-permute-start(bf16[1,64,128]{2,1,0:T(8,128)(2,1)S(1)} %get-tuple-element.18), channel_id=1, source_target_pairs={{0,1},{1,2},{2,3},{3,4},{4,5},{5,6},{6,7},{8,9},{9,10},{10,11},{11... | collective-permute-start | bytes 49160 | tf_op jit(solution)/shard_map/ppermute | solution.py:19
  214.1 6.8 %collective-permute-start.5 = (bf16[1,64,128]{2,1,0:T(8,128)(2,1)S(1)}, bf16[1,64,128]{2,1,0:T(8,128)(2,1)S(1)}, u32[]{:S(2)}, u32[]{:S(2)}) collective-permute-start(bf16[1,64,128]{2,1,0:T(8,128)(2,1)S(1)} %get-tuple-element.17), channel_id=1, source_target_pairs={{1,0},{2,1},{3,2},{4,3},{5,4},{6,5},{7,6},{9,8},{10,9},{11,10},{12... | collective-permute-start | bytes 49160 | tf_op jit(solution)/shard_map/ppermute | solution.py:22
  221.0 2.6 collective-permute-start.6
  222.3 3.3 collective-permute-start.7
  260.6 10.2 %copy-start.6 = (bf16[27,128,128]{2,1,0:T(8,128)(2,1)S(1)}, bf16[27,128,128]{2,1,0:T(8,128)(2,1)}, u32[]{:S(2)}) copy-start(bf16[27,128,128]{2,1,0:T(8,128)(2,1)} %param.19) | copy-start | bytes 2654212
  270.8 84.6 %copy-start.1 = (bf16[1,1,512,128]{3,2,1,0:T(8,128)(2,1)S(1)}, bf16[1,1,512,128]{3,2,1,0:T(8,128)(2,1)}, u32[]{:S(2)}) copy-start(bf16[1,1,512,128]{3,2,1,0:T(8,128)(2,1)} %param.12) | copy-start | bytes 393220
  270.8 84.6 %copy-start.4 = (f32[128]{0:T(128)S(1)}, f32[128]{0:T(128)}, u32[]{:S(2)}) copy-start(f32[128]{0:T(128)} %param.21) | copy-start | bytes 1540
  270.8 84.6 %copy-start.5 = (f32[128]{0:T(128)S(1)}, f32[128]{0:T(128)}, u32[]{:S(2)}) copy-start(f32[128]{0:T(128)} %param.20) | copy-start | bytes 1540
